TPU v7x, 1024 devices: a whole 4x8x16 slice. The times are simulated.
1024 devices in a mesh: seq: 128 (over y, z), tensor: 8 (over x, core).
Axes of the slice: x: 4, y: 8, z: 16, core: 2. Of those that a mesh axis runs over, the one named last changes fastest.
Arguments:
- queries: bfloat16 [12288, 4096], P('seq', 'tensor'), may hold values from -96 to 96
- keys: bfloat16 [12288, 1024], P('seq', 'tensor'), may hold values from -96 to 96
- values: bfloat16 [12288, 1024], P('seq', 'tensor'), may hold values from -6 to 6
- out_weight: bfloat16 [4096, 4096], P('tensor'), may hold values from -0.09375 to 0.09375
- doc_lengths: int32 [16], replicated, may hold values from 1 to 3072, 12288 in all
- stretch_place: int32 [256], replicated, may hold values from 0 to 255, each once
Outputs:
- output: bfloat16 [12288, 4096], P('seq', 'tensor')
Inputs may be any that keep to these rules, and one draw needn't show every extreme that they name: `stretch_place`: each stored block number appears once. `doc_lengths`: the lengths sum to 12288; the longest is exactly 3072.
All inputs are finite; a program needn't handle non-finite values.
Results may differ from a plain program's by a relative error of at most 0.015.
Values may be sent and summed in bfloat16 or wider, within the bound.
No kernel may reach another device: no remote copies, remote signals or barrier semaphores. Data moves between devices by JAX's collectives and lax.ppermute only.
A program may use at most 64 MiB of HBM per device.

v0:
```python
import math

import jax
import jax.numpy as jnp
from jax import lax
from jax.sharding import PartitionSpec as P

HD = 128


rope_base = 500000.0


def sent_together(arrays, axis, dim, along):
    both = jnp.concatenate(arrays, axis=along)
    result, at, gathered = (lax.all_gather(both, axis, axis=dim, tiled=True), 0, [])
    for a in arrays:
        gathered.append(lax.slice_in_dim(result, at, at + a.shape[along], axis=along))
        at += a.shape[along]
    return tuple(gathered)


def in_blocks(value, dim, peers):
    shape = value.shape
    tiles = value.reshape(*shape[:dim], peers, shape[dim] // peers, *shape[dim + 1 :])
    return jnp.moveaxis(tiles, dim, 0)


def sum_at_owner(value, axis, dim):
    tiles = in_blocks(value, dim, lax.axis_size(axis))
    arrived = lax.all_to_all(tiles, axis, split_axis=0, concat_axis=0, tiled=True)
    return arrived.astype(jnp.float32).sum(axis=0)


def seq_positions(first, count, stretch_place, block_rows):
    row_index = first + jnp.arange(count, dtype=jnp.int32)
    return stretch_place[row_index // block_rows] * block_rows + row_index % block_rows


def documents(positions, doc_lengths):
    ends = jnp.cumsum(doc_lengths)
    return jnp.sum((ends[None, :] <= positions[:, None]).astype(jnp.int32), axis=1)


def rotary(heads_in, positions):
    width = heads_in.shape[-1]
    half = width // 2
    freqs = rope_base ** (-(2.0 / width) * jnp.arange(half, dtype=jnp.float32))
    angles = positions.astype(jnp.float32)[:, None] * freqs[None, :]
    cosine = jnp.cos(angles)[:, None, :]
    sine = jnp.sin(angles)[:, None, :]
    floats = heads_in.astype(jnp.float32)
    first_half = floats[..., :half]
    second_half = floats[..., half:]
    rotated = jnp.concatenate(
        [first_half * cosine - second_half * sine, second_half * cosine + first_half * sine],
        axis=-1,
    )
    return rotated.astype(jnp.bfloat16)


def key_block_rows(count):
    for candidate in (512, 384, 256, 192, 128, 96, 64, 48, 32, 16, 8):
        return candidate
    return count


def body(queries, keys, values, out_weight, doc_lengths, stretch_place):
    tok_rows = queries.shape[0]
    block_rows = tok_rows // 2
    head_size = HD
    kv_local = keys.shape[1] // head_size
    q_local = queries.shape[1] // head_size
    group = q_local // kv_local
    device = lax.axis_index("seq")
    own_start = device * tok_rows
    positions = seq_positions(own_start, tok_rows, stretch_place, block_rows)
    document = documents(positions, doc_lengths)
    q_rot = rotary(queries.reshape(tok_rows, q_local, head_size), positions).reshape(
        tok_rows, kv_local, group, head_size
    )
    k_rot = rotary(keys.reshape(tok_rows, kv_local, head_size), positions)
    value_heads = values.reshape(tok_rows, kv_local, head_size)
    scale = 1.0 / math.sqrt(head_size)

    def attend_block(state, key_piece, value_piece, start):
        count = key_piece.shape[0]
        key_positions = seq_positions(start, count, stretch_place, block_rows)
        key_document = documents(key_positions, doc_lengths)
        allowed = (key_positions[None, :] <= positions[:, None]) & (
            key_document[None, :] == document[:, None]
        )
        run_max, run_total, accum = state
        scores = (
            jnp.einsum("tkgd,nkd->kgtn", q_rot, key_piece, preferred_element_type=jnp.float32)
            * scale
        )
        scores = jnp.where(allowed[None, None], scores, -1e30)
        new_max = jnp.maximum(run_max, jnp.max(scores, axis=-1))
        weights = jnp.where(allowed[None, None], jnp.exp(scores - new_max[..., None]), 0.0)
        factor = jnp.exp(run_max - new_max)
        new_total = run_total * factor + jnp.sum(weights, axis=-1)
        update = jnp.einsum(
            "kgtn,nkd->tkgd",
            weights.astype(jnp.bfloat16),
            value_piece,
            preferred_element_type=jnp.float32,
        )
        new_accum = accum * jnp.transpose(factor, (2, 0, 1))[..., None] + update
        return (new_max, new_total, new_accum)

    initial = (
        jnp.full((kv_local, group, tok_rows), -1e30, jnp.float32),
        jnp.zeros((kv_local, group, tok_rows), jnp.float32),
        jnp.zeros((tok_rows, kv_local, group, head_size), jnp.float32),
    )
    key_piece, value_piece = sent_together((k_rot, value_heads), "seq", 0, 1)
    count = key_piece.shape[0]
    step_rows = key_block_rows(count)
    steps_total = count // step_rows
    key_blocks = key_piece.reshape(steps_total, step_rows, kv_local, head_size)
    value_blocks = value_piece.reshape(steps_total, step_rows, kv_local, head_size)

    def one_step(carry, inputs):
        key_block, value_block, offset = inputs
        return (attend_block(carry, key_block, value_block, offset * step_rows), None)

    offsets = jnp.arange(steps_total, dtype=jnp.int32)
    result, unused = lax.scan(one_step, initial, (key_blocks, value_blocks, offsets))
    state = result
    run_max, run_total, accum = state
    attended = (
        (accum / jnp.transpose(run_total, (2, 0, 1))[..., None])
        .astype(jnp.bfloat16)
        .reshape(tok_rows, q_local * head_size)
    )
    partial_rows = jnp.dot(attended, out_weight, preferred_element_type=jnp.float32)
    return sum_at_owner(partial_rows.astype(jnp.bfloat16), "tensor", 1).astype(jnp.bfloat16)


def solution(mesh):
    in_specs = (
        P("seq", "tensor"),
        P("seq", "tensor"),
        P("seq", "tensor"),
        P("tensor", None),
        P(),
        P(),
    )
    out_specs = P("seq", "tensor")
    return jax.shard_map(body, mesh=mesh, in_specs=in_specs, out_specs=out_specs, check_vma=False)
```

profile of v0, /device:TPU:1, one launch (start us, length us, event | category | flops | bytes accessed | tf_op | source)
XLA Modules:
  0.0 375.2 jit_solution(17239565724115446061)
XLA Ops:
  6.6 1.6 gather_fusion.1
  9.2 1.4 pad_maximum_fusion.1
  13.3 152.5 %all-gather.2.cloned.1.call-done = bf16[12288,2,128]{2,0,1:T(8,128)(2,1)} async-done(((bf16[96,2,128]{2,0,1:T(8,128)(2,1)}), bf16[12288,2,128]{2,0,1:T(8,128)(2,1)}) %all-gather.2.cloned.1.call-update) | async-done | bytes 6291472 | tf_op jit(solution)/shard_map/all_gather | solution.py:16
  165.8 4.3 %fusion.40 = (bf16[12288,1,128]{2,0,1:T(8,128)(2,1)S(1)}, bf16[12288,1,128]{2,0,1:T(8,128)(2,1)}) fusion(bf16[12288,2,128]{2,0,1:T(8,128)(2,1)} %all-gather.2.cloned.1.call-done), kind=kLoop, calls=%fused_computation.73 | loop fusion | bytes 12582912 | tf_op jit(solution)/shard_map/slice | solution.py:18
  170.1 168.9 %while.17 = (s32[]{:T(128)}, f32[1,4,96]{2,1,0:T(4,128)S(1)}, f32[1,4,96]{2,1,0:T(4,128)S(1)}, f32[96,1,4,128]{3,0,2,1:T(8,128)S(1)}, s32[24]{0:T(128)S(1)}, /*i...) while((s32[]{:T(128)}, f32[1,4,96]{2,1,0:T(4,128)S(1)}, ...), condition=%wide.region_6.7_spmd.clone, body=%wide.region_2.6_spmd.clone.sunk | while | flops 102765824 | bytes 3362825 | solution.py:129
  171.3 3.5 gather_fusion
  175.1 1.3 fusion.52
  178.4 3.5 gather_fusion
  185.4 3.5 gather_fusion
  192.4 3.5 gather_fusion
  199.5 3.5 gather_fusion
  206.5 3.5 gather_fusion
  213.6 3.5 gather_fusion
  220.6 3.5 gather_fusion
  227.6 3.5 gather_fusion
  234.7 3.5 gather_fusion
  241.7 3.5 gather_fusion
  248.8 3.5 gather_fusion
  255.8 3.5 gather_fusion
  262.8 3.5 gather_fusion
  269.9 3.5 gather_fusion
  276.9 3.5 gather_fusion
  284.0 3.5 gather_fusion
  291.0 3.5 gather_fusion
  298.0 3.5 gather_fusion
  305.1 3.5 gather_fusion
  312.1 3.5 gather_fusion
  319.2 3.5 gather_fusion
  326.2 3.5 gather_fusion
  333.2 3.5 gather_fusion
  339.2 3.0 convolution_convert_fusion
  342.3 25.3 %all_to_all.5 = bf16[8,96,512]{2,1,0:T(8,128)(2,1)S(1)} all-to-all(bf16[8,96,512]{2,1,0:T(8,128)(2,1)S(1)} %bitcast.101), channel_id=1, replica_groups=mesh['seq'=128,'tensor'=8] {'tensor'}, dimensions={0} | all-to-all | bytes 1572864 | tf_op jit(solution)/shard_map/all_to_all | solution.py:31
  (312 shorter events, 70.9 us)
Async XLA Ops:
  6.5 159.2 %all-gather.2.cloned.1.call-start = ((), (), s32[]{:S(2)}) async-start(), calls=%async_computation.1 | async-start | bytes 6340608 | tf_op jit(solution)/shard_map/all_gather | solution.py:16
  13.3 156.8 %copy-start = (s32[256]{0:T(256)S(1)}, s32[256]{0:T(256)}, u32[]{:S(2)}) copy-start(s32[256]{0:T(256)} %param.13) | copy-start | bytes 3076
Sparse Core Ops, SparseCore 0:
  11.5 154.2 all-gather.1
where the time goes:
time: 376 us; the launch traced here: 375 us
  waiting for transfers between devices  153 us (41%)
  local copies, waits for them, and re-layouts  105 us (28%)
  matrix products  42.4 us (11%)
  blocking collectives  25.3 us (7%)
  other arithmetic  18.9 us (5%)
  loops' own time  17.2 us (5%)
  between operations  13.5 us (4%)
    all_gather x1, waiting for transfers between devices, sent_together(): lax.all_gather(both, axis, axis=dim, tiled=True)  152 us
    gather x25, local copies, waits for them, and re-layouts, seq_positions(): stretch_place[row_index // block_rows] * block_rows + row_index % block_rows  85.8 us
    dot_general x24, matrix products, attend_block(): jnp.einsum('tkgd,nkd->kgtn', q_rot, key_piece, preferred_element_type=jnp...  30.4 us
    all_to_all x1, blocking collectives, sum_at_owner(): lax.all_to_all(tiles, axis, split_axis=0, concat_axis=0, tiled=True)  25.3 us
    another operation x1, loops' own time, body(): lax.scan(one_step, initial, (key_blocks, value_blocks, offsets))  17.2 us
    dynamic_slice x24, local copies, waits for them, and re-layouts, body(): lax.scan(one_step, initial, (key_blocks, value_blocks, offsets))  14.1 us
    dot_general x24, matrix products, attend_block(): jnp.einsum('kgtn,nkd->tkgd', weights.astype(jnp.bfloat16), value_piece, p...  8.99 us
    reduce_sum x24, other arithmetic, attend_block(): new_total = run_total * factor + jnp.sum(weights, axis=-1)  7.53 us
  transfers between devices with their start and end apart: 1, of which 1 were waited for; matrix products, arithmetic and copies ran while one was open for 1% of the time, Pallas kernels for 0%

commit v1 on v0

v1 whole, which is shorter than its diff:
```python
import math

import jax
import jax.numpy as jnp
import numpy as np
from jax import lax
from jax.experimental import pallas as pl
from jax.experimental.pallas import tpu as pltpu
from jax.sharding import Mesh
from jax.sharding import PartitionSpec as P

HD = 128
HALF = HD // 2
BLOCK = 48
ROPE_BASE = 500000.0
NEG = -1e30
STAT = 16
SCALE = math.log2(math.e) / math.sqrt(HD)


def rope_tables(blocks):
    freqs = ROPE_BASE ** (-(2.0 / HD) * np.arange(HALF, dtype=np.float64))
    freqs = np.concatenate([freqs, freqs])
    start = (BLOCK * np.arange(blocks, dtype=np.float64))[:, None] * freqs
    row = np.arange(BLOCK, dtype=np.float64)[:, None] * freqs
    f32 = np.float32
    return (np.cos(start).astype(f32), np.sin(start).astype(f32), np.cos(row).astype(f32), np.sin(row).astype(f32))


def rotate_kernel(place, q, k, v, cos_start, sin_start, cos_row, sin_row, q_out, kv_out):
    heads = q.shape[1] // HD
    first = lax.axis_index("y") * lax.axis_size("z") + lax.axis_index("z")
    lane = lax.broadcasted_iota(jnp.int32, (BLOCK, HD), 1)
    for b in range(2):
        at = place[first * 2 + b]
        c0 = cos_start[pl.ds(at, 1), :]
        s0 = sin_start[pl.ds(at, 1), :]
        cosine = c0 * cos_row[...] - s0 * sin_row[...]
        sine = s0 * cos_row[...] + c0 * sin_row[...]
        sine = jnp.where(lane < HALF, -sine, sine)
        rows = pl.ds(b * BLOCK, BLOCK)
        for h in range(heads):
            x = q[rows, pl.ds(h * HD, HD)].astype(jnp.float32)
            y = x * cosine + pltpu.roll(x, HALF, 1) * sine
            q_out[rows, pl.ds(h * HD, HD)] = y.astype(jnp.bfloat16)
        x = k[rows, :].astype(jnp.float32)
        y = x * cosine + pltpu.roll(x, HALF, 1) * sine
        kv_out[rows, pl.ds(0, HD)] = y.astype(jnp.bfloat16)
        kv_out[rows, pl.ds(HD, HD)] = v[rows, :]


def attend_kernel(place, ends, q, kv, out, scores, values_t):
    heads = q.shape[2] // HD
    lanes = 2 * heads * BLOCK
    n_keys = kv.shape[0]
    n_blocks = n_keys // BLOCK
    z_size = lax.axis_size("z")
    my_y = lax.axis_index("y")
    my_z = lax.axis_index("z")
    peer = pl.program_id(0)

    @pl.when(peer == 0)
    def prepare():
        values_t[pl.ds(0, HD), :] = kv[:, pl.ds(HD, HD)].T
        values_t[pl.ds(HD, STAT), :] = jnp.ones((STAT, n_keys), jnp.bfloat16)

    base = (peer * z_size + my_z) * 2
    p0 = place[base] * BLOCK
    p1 = place[base + 1] * BLOCK
    lane = lax.broadcasted_iota(jnp.int32, (8, lanes), 1)
    q_pos = jnp.where(lane < heads * BLOCK, p0, p1) + lane % BLOCK
    q_start = jnp.zeros((8, lanes), jnp.int32)
    end = jnp.int32(0)
    for d in range(ends.shape[0]):
        end = end + ends[d]
        q_start = jnp.where(end <= q_pos, end, q_start)
    parts = []
    for b in range(2):
        for h in range(heads):
            parts.append(q[0, pl.ds(b * BLOCK, BLOCK), pl.ds(h * HD, HD)])
    q_rows = jnp.concatenate(parts, axis=0)
    sub = lax.broadcasted_iota(jnp.int32, (8, lanes), 0)
    top = jnp.full((8, lanes), NEG, jnp.float32)
    for j in range(n_blocks):
        s = lax.dot_general(
            kv[pl.ds(j * BLOCK, BLOCK), pl.ds(0, HD)],
            q_rows,
            (((1,), (1,)), ((), ())),
            preferred_element_type=jnp.float32,
        )
        k0 = place[my_y * n_blocks + j] * BLOCK
        for r in range(0, BLOCK, 8):
            k_pos = sub + (k0 + r)
            piece = jnp.where((k_pos <= q_pos) & (k_pos >= q_start), s[r : r + 8], NEG)
            scores[pl.ds(j * BLOCK + r, 8), :] = piece
            top = jnp.maximum(top, piece)
    top = jnp.max(top, axis=0, keepdims=True)
    safe = jnp.maximum(top, -1e29)
    weights = jnp.exp2((scores[...] - safe) * SCALE).astype(jnp.bfloat16)
    sums = jnp.dot(values_t[...], weights, preferred_element_type=jnp.float32)
    out[0, pl.ds(0, HD), :] = sums[:HD].astype(jnp.bfloat16)
    total = sums[HD : HD + 1]
    t0 = total.astype(jnp.bfloat16)
    t1 = (total - t0.astype(jnp.float32)).astype(jnp.bfloat16)
    m0 = top.astype(jnp.bfloat16)
    rest = top - m0.astype(jnp.float32)
    m1 = rest.astype(jnp.bfloat16)
    m2 = (rest - m1.astype(jnp.float32)).astype(jnp.bfloat16)
    zero = jnp.zeros((STAT - 5, lanes), jnp.bfloat16)
    out[0, pl.ds(HD, STAT), :] = jnp.concatenate([m0, m1, m2, t0, t1, zero], axis=0)


def project_kernel(parts, weight, out, rows):
    heads = rows.shape[1] // HD
    peers = parts.shape[0]

    @pl.when(pl.program_id(0) == 0)
    def combine():
        tops, totals = [], []
        for p in range(peers):
            stat = parts[p, pl.ds(HD, STAT), :].astype(jnp.float32)
            tops.append(stat[0:1] + stat[1:2] + stat[2:3])
            totals.append(stat[3:4] + stat[4:5])
        top = tops[0]
        for p in range(1, peers):
            top = jnp.maximum(top, tops[p])
        total = jnp.zeros_like(top)
        factors = []
        for p in range(peers):
            factor = jnp.exp2((tops[p] - top) * SCALE)
            total = total + factor * totals[p]
            factors.append(factor)
        total = 1.0 / total
        mixed = jnp.zeros((HD, top.shape[1]), jnp.float32)
        for p in range(peers):
            mixed = mixed + parts[p, pl.ds(0, HD), :].astype(jnp.float32) * (factors[p] * total)
        turned = mixed.T.astype(jnp.bfloat16)
        for b in range(2):
            for h in range(heads):
                at = (b * heads + h) * BLOCK
                rows[pl.ds(b * BLOCK, BLOCK), pl.ds(h * HD, HD)] = turned[at : at + BLOCK]

    out[0] = jnp.dot(rows[...], weight[...], preferred_element_type=jnp.float32).astype(jnp.bfloat16)


SMEM = pl.BlockSpec(memory_space=pltpu.SMEM)


def body(queries, keys, values, out_weight, doc_lengths, stretch_place):
    tok, q_width = queries.shape
    heads = q_width // HD
    ny, nz, nt = lax.axis_size("y"), lax.axis_size("z"), lax.axis_size("tensor")
    lanes = 2 * heads * BLOCK
    bf16 = jnp.bfloat16
    tables = [jnp.asarray(t) for t in rope_tables(stretch_place.shape[0])]
    vmem = pl.BlockSpec(memory_space=pltpu.VMEM)
    q_rot, kv = pl.pallas_call(
        rotate_kernel,
        out_shape=(jax.ShapeDtypeStruct((tok, q_width), bf16), jax.ShapeDtypeStruct((tok, 2 * HD), bf16)),
        in_specs=[SMEM] + [vmem] * 7,
        out_specs=(vmem, vmem),
        compiler_params=pltpu.CompilerParams(vmem_limit_bytes=8 << 20),
        name="rotate",
    )(stretch_place, queries, keys, values, *tables)
    kv_all = lax.all_gather(kv, "z", axis=0, tiled=True)
    q_all = gather_queries(q_rot, ny)
    n_keys = nz * tok
    parts = pl.pallas_call(
        attend_kernel,
        out_shape=jax.ShapeDtypeStruct((ny, HD + STAT, lanes), bf16),
        grid=(ny,),
        in_specs=[
            SMEM,
            SMEM,
            pl.BlockSpec((1, tok, q_width), lambda i: (i, 0, 0)),
            pl.BlockSpec((n_keys, 2 * HD), lambda i: (0, 0)),
        ],
        out_specs=pl.BlockSpec((1, HD + STAT, lanes), lambda i: (i, 0, 0)),
        scratch_shapes=[pltpu.VMEM((n_keys, lanes), jnp.float32), pltpu.VMEM((HD + STAT, n_keys), bf16)],
        compiler_params=pltpu.CompilerParams(vmem_limit_bytes=20 << 20),
        name="attend",
    )(stretch_place, doc_lengths, q_all, kv_all)
    parts = lax.all_to_all(parts, "y", split_axis=0, concat_axis=0, tiled=True)
    model = out_weight.shape[1]
    step = model // nt
    partial_rows = pl.pallas_call(
        project_kernel,
        out_shape=jax.ShapeDtypeStruct((nt, tok, step), bf16),
        grid=(nt,),
        in_specs=[
            pl.BlockSpec((ny, HD + STAT, lanes), lambda i: (0, 0, 0)),
            pl.BlockSpec((q_width, step), lambda i: (0, i)),
        ],
        out_specs=pl.BlockSpec((1, tok, step), lambda i: (i, 0, 0)),
        scratch_shapes=[pltpu.VMEM((tok, q_width), bf16)],
        compiler_params=pltpu.CompilerParams(vmem_limit_bytes=12 << 20),
        name="project",
    )(parts, out_weight)
    arrived = lax.all_to_all(partial_rows, "tensor", split_axis=0, concat_axis=0, tiled=True)
    return arrived.astype(jnp.float32).sum(axis=0).astype(bf16)


def gather_queries(q_rot, peers):
    same = jnp.broadcast_to(q_rot[None], (peers,) + q_rot.shape)
    return lax.all_to_all(same, "y", split_axis=0, concat_axis=0, tiled=True)


def solution(mesh, ny=8):
    n_seq, n_tensor = mesh.devices.shape
    inner = Mesh(mesh.devices.reshape(ny, n_seq // ny, n_tensor), ("y", "z", "tensor"))
    seq = ("y", "z")
    in_specs = (P(seq, "tensor"), P(seq, "tensor"), P(seq, "tensor"), P("tensor", None), P(), P())
    return jax.shard_map(body, mesh=inner, in_specs=in_specs, out_specs=P(seq, "tensor"), check_vma=False)
```

time: 376 us -> 129 us (0.34)
  waiting for transfers between devices: 153 us -> 0.01 us
  local copies, waits for them, and re-layouts: 105 us -> 8.62 us
  blocking collectives: 25.3 us -> 89.7 us
  matrix products: 42.4 us -> 0 us
  Pallas kernels: 0 us -> 21.7 us
  other arithmetic: 18.9 us -> 0.76 us
  loops' own time: 17.2 us -> 0 us
  between operations: 13.5 us -> 0.03 us
  starting transfers between devices: 0.01 us -> 7.64 us
    all_gather x1 -> x0, waiting for transfers between devices: 152 us -> none  [sent_together(): lax.all_gather(both, axis, axis=dim, tiled=True)]
    gather x25 -> x0, local copies, waits for them, and re-layouts: 85.8 us -> none  [seq_positions(): stretch_place[row_index // block_rows] * block_rows + row_index % block_rows]
    dot_general x49 -> x0, matrix products: 42.4 us -> none  [the longest x24 30.4 us: attend_block(): jnp.einsum('tkgd,nkd->kgtn', q_rot, key_piece, preferred_element_type=jnp...]
    all_gather x0 -> x1, blocking collectives: none -> 40.8 us  [body(): kv_all = lax.all_gather(kv, 'z', axis=0, tiled=True)]
    all_to_all x1 -> x2, blocking collectives: 25.3 us -> 48.8 us  [the longest x1 25.4 us: body(): lax.all_to_all(partial_rows, 'tensor', split_axis=0, concat_axis=0, tiled...]
    pallas_call x0 -> x3, Pallas kernels: none -> 21.7 us  [the longest x1 18.6 us: body(): pl.pallas_call(attend_kernel, out_shape=jax.ShapeDtypeStruct((ny, HD + ST...]
    another operation x1 -> x0, loops' own time: 17.2 us -> none  [body(): lax.scan(one_step, initial, (key_blocks, value_blocks, offsets))]
    dynamic_slice x24 -> x0, local copies, waits for them, and re-layouts: 14.1 us -> none  [body(): lax.scan(one_step, initial, (key_blocks, value_blocks, offsets))]
  transfers between devices with their start and end apart: 1 -> 1, of which waited for: 1 -> 0; matrix products, arithmetic and copies ran while one was open for 1% -> 0% of each run, Pallas kernels for 0% -> 0%
where the time goes in v1:
time: 129 us; the launch traced here: 128 us
  blocking collectives  89.7 us (70%)
  Pallas kernels  21.7 us (17%)
  local copies, waits for them, and re-layouts  8.62 us (7%)
  starting transfers between devices  7.64 us (6%)
    all_gather x1, blocking collectives, body(): kv_all = lax.all_gather(kv, 'z', axis=0, tiled=True)  40.8 us
    all_to_all x1, blocking collectives, body(): lax.all_to_all(partial_rows, 'tensor', split_axis=0, concat_axis=0, tiled...  25.4 us
    all_to_all x1, blocking collectives, body(): parts = lax.all_to_all(parts, 'y', split_axis=0, concat_axis=0, tiled=True)  23.4 us
    pallas_call x1, Pallas kernels, body(): pl.pallas_call(attend_kernel, out_shape=jax.ShapeDtypeStruct((ny, HD + ST...  18.6 us
    unnamed x22, local copies, waits for them, and re-layouts  7.66 us
    all_to_all x1, starting transfers between devices, gather_queries(): return lax.all_to_all(same, 'y', split_axis=0, concat_axis=0, tiled=True)  7.64 us
  transfers between devices with their start and end apart: 1, of which 0 were waited for; matrix products, arithmetic and copies ran while one was open for 0% of the time, Pallas kernels for 0%

profile of v1, /device:TPU:1, one launch (start us, length us, event | category | flops | bytes accessed | tf_op | source)
XLA Modules:
  0.0 128.4 jit_solution(14204803167976582861)
XLA Ops:
  0.0 0.0 copy-start.1
  0.0 0.9 copy-done.1
  0.9 0.0 copy-start.2
  0.9 0.9 copy-done.2
  1.8 0.0 copy-start.3
  1.8 0.9 copy-done.3
  2.7 0.0 copy-start.4
  2.7 0.7 copy-done.4
  3.4 0.0 copy-start.5
  3.4 0.7 copy-done.5
  4.2 0.0 copy-start.6
  4.2 0.7 copy-done.6
  4.9 0.0 copy-start.7
  4.9 0.7 copy-done.7
  5.7 0.0 copy-start.8
  5.7 0.7 copy-done.8
  6.3 0.7 rotate.1
  7.0 1.0 broadcast_in_dim.2
  8.0 7.6 %all-to-all-start = ((bf16[8,96,512]{2,1,0:T(8,128)(2,1)}), bf16[8,96,512]{2,1,0:T(8,128)(2,1)S(1)}, u32[]{:S(2)}, u32[]{:S(2)}) async-start(bf16[8,96,512]{2,1,0:T(8,128)(2,1)} %broadcast_in_dim.2), calls=%async_computation | async-start | bytes 1572864 | tf_op jit(solution)/shard_map/all_to_all | solution.py:205
  15.6 40.8 %all_gather.3.kv = bf16[1536,256]{1,0:T(8,128)(2,1)S(1)} all-gather(bf16[96,256]{1,0:T(8,128)(2,1)S(1)} %get-tuple-element.8), channel_id=1, replica_groups=mesh['y'=8,'z'=16,'tensor'=8] {'z'}, dimensions={0}, use_global_device_ids=true | all-gather | bytes 835584 | tf_op jit(solution)/shard_map/all_gather | solution.py:165
  56.4 0.0 all-to-all-done.q
  56.4 0.0 copy-start.9
  56.4 0.7 copy-done.9
  57.1 0.0 copy-start.10
  57.1 0.7 copy-done.10
  57.8 0.0 copy-start
  57.8 18.6 %attend.1 = bf16[8,144,384]{2,1,0:T(8,128)(2,1)S(1)} custom-call(s32[256]{0:T(256)S(1)} %copy-done.9, s32[16]{0:T(128)S(1)} %copy-done.10, bf16[8,96,512]{2,1,0:T(8,128)(2,1)S(1)} %all-to-all-done.q, bf16[1536,256]{1,0:T(8,128)(2,1)S(1)} %all_gather.3.kv), custom_call_target="tpu_custom_call" | custom-call | tf_op jit(solution)/shard_map/attend/pallas_call | solution.py:168
  76.3 23.4 %all_to_all.15.parts = bf16[8,144,384]{2,1,0:T(8,128)(2,1)S(1)} all-to-all(bf16[8,144,384]{2,1,0:T(8,128)(2,1)S(1)} %attend.1), channel_id=1, replica_groups=mesh['y'=8,'z'=16,'tensor'=8] {'y'}, dimensions={0} | all-to-all | bytes 1769472 | tf_op jit(solution)/shard_map/all_to_all | solution.py:183
  99.8 0.0 copy-done
  99.8 2.4 %project.1 = bf16[8,96,512]{2,1,0:T(8,128)(2,1)S(1)} custom-call(bf16[8,144,384]{2,1,0:T(8,128)(2,1)S(1)} %all_to_all.15.parts, bf16[512,4096]{1,0:T(8,128)(2,1)S(1)} %copy-done), custom_call_target="tpu_custom_call" | custom-call | tf_op jit(solution)/shard_map/project/pallas_call | solution.py:186
  102.2 25.4 %all_to_all.16 = bf16[8,96,512]{2,1,0:T(8,128)(2,1)S(1)} all-to-all(bf16[8,96,512]{2,1,0:T(8,128)(2,1)S(1)} %project.1), channel_id=1, replica_groups=mesh['y'=8,'z'=16,'tensor'=8] {'tensor'}, dimensions={0} | all-to-all | bytes 1572864 | tf_op jit(solution)/shard_map/all_to_all | solution.py:199
  127.6 0.8 reduce_sum.12
Async XLA Ops:
  0.0 0.9 copy-start.1
  0.9 0.9 copy-start.2
  1.8 0.9 copy-start.3
  2.7 0.7 copy-start.4
  3.4 0.7 copy-start.5
  4.2 0.7 copy-start.6
  4.9 0.7 copy-start.7
  5.7 0.7 copy-start.8
  8.0 48.5 %all-to-all-start = ((bf16[8,96,512]{2,1,0:T(8,128)(2,1)}), bf16[8,96,512]{2,1,0:T(8,128)(2,1)S(1)}, u32[]{:S(2)}, u32[]{:S(2)}) async-start(bf16[8,96,512]{2,1,0:T(8,128)(2,1)} %broadcast_in_dim.2), calls=%async_computation | async-start | bytes 1572864 | tf_op jit(solution)/shard_map/all_to_all | solution.py:205
  56.4 0.7 copy-start.9
  57.1 0.7 copy-start.10
  57.8 42.0 %copy-start = (bf16[512,4096]{1,0:T(8,128)(2,1)S(1)}, bf16[512,4096]{1,0:T(8,128)(2,1)}, u32[]{:S(2)}) copy-start(bf16[512,4096]{1,0:T(8,128)(2,1)} %weight.1) | copy-start | bytes 12582916

commit v2 on v1

v2 whole, which is shorter than its diff:
```python
import math

import jax
import jax.numpy as jnp
import numpy as np
from jax import lax
from jax.experimental import pallas as pl
from jax.experimental.pallas import tpu as pltpu
from jax.sharding import Mesh
from jax.sharding import PartitionSpec as P

HD = 128
HALF = HD // 2
BLOCK = 48
ROPE_BASE = 500000.0
BIG = 2.0**100
FLOOR = -1e29
FAR = 1 << 30
STAT = 16
CHUNK = 512
SCALE = math.log2(math.e) / math.sqrt(HD)
BF16 = jnp.bfloat16
F32 = jnp.float32


def rope_tables(blocks):
    freqs = ROPE_BASE ** (-(2.0 / HD) * np.arange(HALF, dtype=np.float64))
    freqs = np.concatenate([freqs, freqs])
    start = (BLOCK * np.arange(blocks, dtype=np.float64))[:, None] * freqs
    row = np.arange(BLOCK, dtype=np.float64)[:, None] * freqs
    return np.concatenate([np.cos(row), np.sin(row), np.cos(start), np.sin(start)]).astype(np.float32)


def rotate_kernel(place_in, q_in, k_in, v_in, table_in, q_out, kv_out, place, q, k, v, table, sems):
    sources = (place_in, table_in, q_in, k_in, v_in)
    copies = [pltpu.make_async_copy(s, d, sems.at[i]) for i, (s, d) in enumerate(zip(sources, (place, table, q, k, v)))]
    for copy in copies:
        copy.start()
    for copy in copies:
        copy.wait()
    heads = q.shape[1] // HD
    blocks = place.shape[0]
    first = lax.axis_index("y") * lax.axis_size("z") + lax.axis_index("z")
    lane = lax.broadcasted_iota(jnp.int32, (BLOCK, HD), 1)
    cos_row = table[pl.ds(0, BLOCK), :]
    sin_row = table[pl.ds(BLOCK, BLOCK), :]
    for b in range(2):
        at = place[first * 2 + b]
        c0 = table[pl.ds(2 * BLOCK + at, 1), :]
        s0 = table[pl.ds(2 * BLOCK + blocks + at, 1), :]
        cosine = c0 * cos_row - s0 * sin_row
        sine = s0 * cos_row + c0 * sin_row
        sine = jnp.where(lane < HALF, -sine, sine)
        rows = pl.ds(b * BLOCK, BLOCK)
        for h in range(heads):
            x = q[rows, pl.ds(h * HD, HD)].astype(F32)
            y = (x * cosine + pltpu.roll(x, HALF, 1) * sine).astype(BF16)
            for p in range(q_out.shape[0]):
                q_out[p, rows, pl.ds(h * HD, HD)] = y
        x = k[rows, :].astype(F32)
        y = x * cosine + pltpu.roll(x, HALF, 1) * sine
        kv_out[rows, pl.ds(0, HD)] = y.astype(BF16)
        kv_out[rows, pl.ds(HD, HD)] = v[rows, :]


def attend_kernel(place_in, docs_in, q, kv, out, place, docs, scores, values_t, keys, queries, sems):
    copies = [
        pltpu.make_async_copy(place_in, place, sems.at[0]),
        pltpu.make_async_copy(docs_in, docs, sems.at[1]),
    ]
    for copy in copies:
        copy.start()
    peers, tok, width = q.shape
    heads = width // HD
    lanes = 2 * heads * BLOCK
    n_keys = kv.shape[0]
    n_blocks = n_keys // BLOCK
    n_docs = docs.shape[0]
    z_size = lax.axis_size("z")
    my_y = lax.axis_index("y")
    my_z = lax.axis_index("z")
    values_t[pl.ds(0, HD), :] = kv[:, pl.ds(HD, HD)].T
    values_t[pl.ds(HD, STAT), :] = jnp.ones((STAT, n_keys), BF16)
    keys[:, pl.ds(0, HD)] = kv[:, pl.ds(0, HD)]
    for copy in copies:
        copy.wait()

    lane = lax.broadcasted_iota(jnp.int32, (1, HD), 1)
    begin = jnp.full((1, HD), FAR, jnp.int32)
    end = jnp.full((1, HD), FAR, jnp.int32)
    edge = jnp.int32(0)
    for d in range(n_docs):
        begin = jnp.where(lane == d, edge, begin)
        edge = edge + docs[d]
        end = jnp.where(lane == d, edge, end)
    causal_at = n_docs
    own_at = causal_at + 2 * peers
    assert own_at + 2 * BLOCK <= HD
    for p in range(peers):
        for b in range(2):
            after = (place[(p * z_size + my_z) * 2 + b] + 1) * BLOCK
            begin = jnp.where(lane == causal_at + 2 * p + b, after, begin)
    for b in range(2):
        at = own_at + b * BLOCK
        mine = (lane >= at) & (lane < at + BLOCK)
        key_at = place[(my_y * z_size + my_z) * 2 + b] * BLOCK + lane - at
        begin = jnp.where(mine, key_at, begin)
        end = jnp.where(mine, key_at + 1, end)

    row = lax.broadcasted_iota(jnp.int32, (BLOCK, HD), 0)
    wide = lax.broadcasted_iota(jnp.int32, (BLOCK, HD), 1)

    def key_columns(j, _):
        k_pos = row + place[my_y * n_blocks + j] * BLOCK
        inside = (k_pos >= begin) & (k_pos < end)
        at = pl.multiple_of(j * BLOCK, BLOCK)
        keys[pl.ds(at, BLOCK), pl.ds(HD, HD)] = jnp.where(inside, -BIG, 0.0).astype(BF16)
        return 0

    lax.fori_loop(0, n_blocks, key_columns, 0, unroll=4)

    def one_peer(p, _):
        for b in range(2):
            q_pos = row + place[(p * z_size + my_z) * 2 + b] * BLOCK
            doc = jnp.where((q_pos < begin) | (q_pos >= end), 1.0, 0.0)
            block = jnp.where((q_pos >= begin - BLOCK) & (q_pos < begin), 1.0, 0.0)
            later = jnp.where(q_pos < begin, 1.0, 0.0)
            columns = jnp.where(wide < causal_at, doc, jnp.where(wide < own_at, block, later)).astype(BF16)
            for h in range(heads):
                rows = pl.ds((b * heads + h) * BLOCK, BLOCK)
                queries[rows, pl.ds(0, HD)] = q[p, pl.ds(b * BLOCK, BLOCK), pl.ds(h * HD, HD)]
                queries[rows, pl.ds(HD, HD)] = columns
        top = jnp.full((8, lanes), -4.0 * BIG, F32)
        for at in range(0, n_keys, CHUNK):
            size = min(CHUNK, n_keys - at)
            s = lax.dot_general(
                keys[pl.ds(at, size), :],
                queries[...],
                (((1,), (1,)), ((), ())),
                preferred_element_type=F32,
            )
            scores[pl.ds(at, size), :] = s
            top = jnp.maximum(top, jnp.max(s.reshape(size // 8, 8, lanes), axis=0))
        top = jnp.max(top, axis=0, keepdims=True)
        safe = jnp.maximum(top, FLOOR)
        sums = jnp.zeros((HD + STAT, lanes), F32)
        for at in range(0, n_keys, CHUNK):
            size = min(CHUNK, n_keys - at)
            weights = jnp.exp2((scores[pl.ds(at, size), :] - safe) * SCALE).astype(BF16)
            sums = sums + jnp.dot(values_t[:, pl.ds(at, size)], weights, preferred_element_type=F32)
        out[p, pl.ds(0, HD), :] = sums[:HD].astype(BF16)
        total = sums[HD : HD + 1]
        t0 = total.astype(BF16)
        t1 = (total - t0.astype(F32)).astype(BF16)
        m0 = top.astype(BF16)
        rest = top - m0.astype(F32)
        m1 = rest.astype(BF16)
        m2 = (rest - m1.astype(F32)).astype(BF16)
        zero = jnp.zeros((STAT - 5, lanes), BF16)
        out[p, pl.ds(HD, STAT), :] = jnp.concatenate([m0, m1, m2, t0, t1, zero], axis=0)
        return 0

    lax.fori_loop(0, peers, one_peer, 0)


def combine_kernel(parts, weight, rows, given):
    heads = rows.shape[1] // HD
    peers = parts.shape[0]
    tops, totals = [], []
    for p in range(peers):
        stat = parts[p, pl.ds(HD, STAT), :].astype(F32)
        tops.append(stat[0:1] + stat[1:2] + stat[2:3])
        totals.append(stat[3:4] + stat[4:5])
    top = tops[0]
    for p in range(1, peers):
        top = jnp.maximum(top, tops[p])
    total = jnp.zeros_like(top)
    factors = []
    for p in range(peers):
        factor = jnp.exp2((tops[p] - top) * SCALE)
        total = total + factor * totals[p]
        factors.append(factor)
    total = 1.0 / total
    factors = [f * total for f in factors]
    mixed = parts[0, pl.ds(0, HD), :].astype(F32) * factors[0]
    for p in range(1, peers):
        mixed = mixed + parts[p, pl.ds(0, HD), :].astype(F32) * factors[p]
    turned = mixed.T.astype(BF16)
    for b in range(2):
        for h in range(heads):
            at = (b * heads + h) * BLOCK
            rows[pl.ds(b * BLOCK, BLOCK), pl.ds(h * HD, HD)] = turned[at : at + BLOCK]
    project(rows, weight, given, 1 - lax.axis_index("c"))


def keep_kernel(rows, weight, kept):
    project(rows, weight, kept, lax.axis_index("c"))


def project(rows, weight, out, core):
    step = out.shape[2]
    for x in range(out.shape[0]):
        columns = pl.ds(pl.multiple_of((2 * x + core) * step, step), step)
        out[x] = jnp.dot(rows[...], weight[:, columns], preferred_element_type=F32).astype(out.dtype)


def body(queries, keys, values, out_weight, doc_lengths, stretch_place):
    tok, q_width = queries.shape
    heads = q_width // HD
    ny, nz, nx = lax.axis_size("y"), lax.axis_size("z"), lax.axis_size("x")
    lanes = 2 * heads * BLOCK
    table = rope_tables(stretch_place.shape[0])
    vmem = pl.BlockSpec(memory_space=pltpu.VMEM)
    hbm = pl.BlockSpec(memory_space=pltpu.HBM)
    n_place = stretch_place.shape[0]
    n_docs = doc_lengths.shape[0]
    q_rot, kv = pl.pallas_call(
        rotate_kernel,
        out_shape=(jax.ShapeDtypeStruct((ny, tok, q_width), BF16), jax.ShapeDtypeStruct((tok, 2 * HD), BF16)),
        in_specs=[hbm] * 5,
        out_specs=(vmem, vmem),
        scratch_shapes=[
            pltpu.SMEM((n_place,), jnp.int32),
            pltpu.VMEM((tok, q_width), BF16),
            pltpu.VMEM((tok, HD), BF16),
            pltpu.VMEM((tok, HD), BF16),
            pltpu.VMEM(table.shape, F32),
            pltpu.SemaphoreType.DMA((5,)),
        ],
        compiler_params=pltpu.CompilerParams(vmem_limit_bytes=4 << 20),
        name="rotate",
    )(*[pltpu.with_memory_space_constraint(a, pltpu.HBM) for a in (stretch_place, queries, keys, values, jnp.asarray(table))])
    q_all = lax.all_to_all(q_rot, "y", split_axis=0, concat_axis=0, tiled=True)
    kv_all = lax.all_gather(kv, "z", axis=0, tiled=True)
    n_keys = nz * tok
    pairs = ny * lanes * n_keys
    parts = pl.pallas_call(
        attend_kernel,
        out_shape=jax.ShapeDtypeStruct((ny, HD + STAT, lanes), BF16),
        in_specs=[hbm, hbm, vmem, vmem],
        out_specs=vmem,
        scratch_shapes=[
            pltpu.SMEM((n_place,), jnp.int32),
            pltpu.SMEM((n_docs,), jnp.int32),
            pltpu.VMEM((n_keys, lanes), F32),
            pltpu.VMEM((HD + STAT, n_keys), BF16),
            pltpu.VMEM((n_keys, 2 * HD), BF16),
            pltpu.VMEM((lanes, 2 * HD), BF16),
            pltpu.SemaphoreType.DMA((2,)),
        ],
        compiler_params=pltpu.CompilerParams(vmem_limit_bytes=16 << 20),
        cost_estimate=pl.CostEstimate(flops=4 * pairs * HD, bytes_accessed=4 << 20, transcendentals=pairs),
        name="attend",
    )(
        pltpu.with_memory_space_constraint(stretch_place, pltpu.HBM),
        pltpu.with_memory_space_constraint(doc_lengths, pltpu.HBM),
        q_all,
        kv_all,
    )
    parts = lax.all_to_all(parts, "y", split_axis=0, concat_axis=0, tiled=True)
    step = out_weight.shape[1] // (2 * nx)
    half_flops = 2 * tok * q_width * nx * step
    cost = pl.CostEstimate(flops=half_flops, bytes_accessed=4 << 20, transcendentals=0)
    rows, given = pl.pallas_call(
        combine_kernel,
        out_shape=(jax.ShapeDtypeStruct((tok, q_width), BF16), jax.ShapeDtypeStruct((nx, tok, step), BF16)),
        in_specs=[vmem, vmem],
        out_specs=(vmem, vmem),
        compiler_params=pltpu.CompilerParams(vmem_limit_bytes=8 << 20),
        cost_estimate=cost,
        name="combine",
    )(parts, out_weight)
    got = lax.ppermute(given, "c", [(0, 1), (1, 0)])
    kept = pl.pallas_call(
        keep_kernel,
        out_shape=jax.ShapeDtypeStruct((nx, tok, step), F32),
        in_specs=[vmem, vmem],
        out_specs=vmem,
        compiler_params=pltpu.CompilerParams(vmem_limit_bytes=8 << 20),
        cost_estimate=cost,
        name="keep",
    )(rows, out_weight)
    both = (kept + got.astype(F32)).astype(BF16)
    arrived = lax.all_to_all(both, "x", split_axis=0, concat_axis=0, tiled=True)
    return arrived.astype(F32).sum(axis=0).astype(BF16)


def solution(mesh, ny=8):
    n_seq, n_tensor = mesh.devices.shape
    shape = (ny, n_seq // ny, n_tensor // 2, 2)
    inner = Mesh(mesh.devices.reshape(shape), ("y", "z", "x", "c"))
    seq, tensor = ("y", "z"), ("x", "c")
    split = P(seq, tensor)
    in_specs = (split, split, split, P(tensor, None), P(), P())
    return jax.shard_map(body, mesh=inner, in_specs=in_specs, out_specs=split, check_vma=False)
```

time: 129 us -> 111 us (0.86)
  blocking collectives: 89.7 us -> 75.3 us
  starting transfers between devices: 7.64 us -> 18.8 us
  local copies, waits for them, and re-layouts: 8.62 us -> 0.01 us
  Pallas kernels: 21.7 us -> 15.1 us
    all_to_all x1, blocking collectives: 25.4 us -> 11 us  [body(): arrived = lax.all_to_all(both, 'x', split_axis=0, concat_axis=0, tiled=True)]
    ppermute x0 -> x1, starting transfers between devices: none -> 11.1 us  [body(): got = lax.ppermute(given, 'c', [(0, 1), (1, 0)])]
    unnamed x22 -> x2, local copies, waits for them, and re-layouts: 7.66 us -> 0.01 us
    pallas_call x1, Pallas kernels: 18.6 us -> 11.8 us  [body(): pl.pallas_call(attend_kernel, out_shape=jax.ShapeDtypeStruct((ny, HD + ST...]
    pallas_call x2 -> x3, Pallas kernels: 3.07 us -> 3.27 us  [the longest x1 2.1 us: body(): pl.pallas_call(rotate_kernel, out_shape=(jax.ShapeDtypeStruct((ny, tok, q...]
  transfers between devices with their start and end apart: 1 -> 2, of which waited for: 0 -> 1; matrix products, arithmetic and copies ran while one was open for 0% -> 0% of each run, Pallas kernels for 0% -> 0%
where the time goes in v2:
time: 111 us
  blocking collectives  75.3 us (68%)
  starting transfers between devices  18.8 us (17%)
  Pallas kernels  15.1 us (14%)
    all_gather x1, blocking collectives, body(): kv_all = lax.all_gather(kv, 'z', axis=0, tiled=True)  40.8 us
    all_to_all x1, blocking collectives, body(): parts = lax.all_to_all(parts, 'y', split_axis=0, concat_axis=0, tiled=True)  23.4 us
    pallas_call x1, Pallas kernels, body(): pl.pallas_call(attend_kernel, out_shape=jax.ShapeDtypeStruct((ny, HD + ST...  11.8 us
    ppermute x1, starting transfers between devices, body(): got = lax.ppermute(given, 'c', [(0, 1), (1, 0)])  11.1 us
    all_to_all x1, blocking collectives, body(): arrived = lax.all_to_all(both, 'x', split_axis=0, concat_axis=0, tiled=True)  11 us
    all_to_all x1, starting transfers between devices, body(): q_all = lax.all_to_all(q_rot, 'y', split_axis=0, concat_axis=0, tiled=True)  7.65 us
  transfers between devices with their start and end apart: 2, of which 1 were waited for; matrix products, arithmetic and copies ran while one was open for 0% of the time, Pallas kernels for 0%

profile of v2, /device:TPU:1, one launch (start us, length us, event | category | flops | bytes accessed | tf_op | source)
XLA Modules:
  0.0 110.9 jit_solution(13198404949862789489)
XLA Ops:
  0.0 2.1 %rotate.1 = (bf16[8,96,512]{2,1,0:T(8,128)(2,1)}, bf16[96,256]{1,0:T(8,128)(2,1)S(1)}) custom-call(s32[256]{0:T(256)} %place_in.3, bf16[96,512]{1,0:T(8,128)(2,1)} %q_in.1, bf16[96,128]{1,0:T(8,128)(2,1)} %k_in.1, bf16[96,128]{1,0:T(8,128)(2,1)} %v_in.1, f32[608,128]{1,0:T(8,128)} %constant.5.clone.table_in), custom_call_target="tpu_custom_call" | custom-call | tf_op jit(solution)/shard_map/rotate/pallas_call | solution.py:217
  2.1 7.7 %all-to-all-start = ((bf16[8,96,512]{2,1,0:T(8,128)(2,1)}), bf16[8,96,512]{2,1,0:T(8,128)(2,1)S(1)}, u32[]{:S(2)}, u32[]{:S(2)}) async-start(bf16[8,96,512]{2,1,0:T(8,128)(2,1)} %get-tuple-element.9), calls=%async_computation | async-start | bytes 1572864 | tf_op jit(solution)/shard_map/all_to_all | solution.py:233
  9.8 40.8 %all_gather.3.kv = bf16[1536,256]{1,0:T(8,128)(2,1)S(1)} all-gather(bf16[96,256]{1,0:T(8,128)(2,1)S(1)} %get-tuple-element.10), channel_id=1, replica_groups=mesh['y'=8,'z'=16,'x'=4,'c'=2] {'z'}, dimensions={0}, use_global_device_ids=true | all-gather | bytes 835584 | tf_op jit(solution)/shard_map/all_gather | solution.py:234
  50.6 0.0 all-to-all-done.q
  50.6 0.0 copy-start
  50.6 11.8 %attend.1 = bf16[8,144,384]{2,1,0:T(8,128)(2,1)S(1)} custom-call(s32[256]{0:T(256)} %place_in.3, s32[16]{0:T(128)} %docs_in.1, bf16[8,96,512]{2,1,0:T(8,128)(2,1)S(1)} %all-to-all-done.q, bf16[1536,256]{1,0:T(8,128)(2,1)S(1)} %all_gather.3.kv), custom_call_target="tpu_custom_call" | custom-call | flops 2415919104 | bytes 4194304 | tf_op jit(solution)/shard_map/attend/pallas_call | solution.py:237
  62.4 23.4 %all_to_all.15.parts = bf16[8,144,384]{2,1,0:T(8,128)(2,1)S(1)} all-to-all(bf16[8,144,384]{2,1,0:T(8,128)(2,1)S(1)} %attend.1), channel_id=1, replica_groups=mesh['y'=8,'z'=16,'x'=4,'c'=2] {'y'}, dimensions={0} | all-to-all | bytes 1769472 | tf_op jit(solution)/shard_map/all_to_all | solution.py:260
  85.8 0.0 copy-done
  85.8 0.7 combine.1
  86.5 11.1 %collective-permute-start = (bf16[4,96,512]{2,1,0:T(8,128)(2,1)S(1)}, bf16[4,96,512]{2,1,0:T(8,128)(2,1)S(1)}, u32[]{:S(2)}, u32[]{:S(2)}) collective-permute-start(bf16[4,96,512]{2,1,0:T(8,128)(2,1)S(1)} %get-tuple-element.12), channel_id=1, source_target_pairs={{0,1},{1,0},{2,3},{3,2},{4,5},{5,4},{6,7},{7,6},{8,9},{9,8},{10,11... | collective-permute-start | bytes 1179656 | tf_op jit(solution)/shard_map/ppermute | solution.py:273
  97.7 0.5 keep.1
  98.1 0.9 collective-permute-done
  99.0 0.1 add_convert_fusion
  99.1 11.0 %all_to_all.16 = bf16[4,96,512]{2,1,0:T(8,128)(2,1)S(1)} all-to-all(bf16[4,96,512]{2,1,0:T(8,128)(2,1)S(1)} %add_convert_fusion), channel_id=1, replica_groups=mesh['y'=8,'z'=16,'x'=4,'c'=2] {'x'}, dimensions={0} | all-to-all | bytes 786432 | tf_op jit(solution)/shard_map/all_to_all | solution.py:284
  110.2 0.7 reduce_sum.12
Async XLA Ops:
  2.1 48.5 %all-to-all-start = ((bf16[8,96,512]{2,1,0:T(8,128)(2,1)}), bf16[8,96,512]{2,1,0:T(8,128)(2,1)S(1)}, u32[]{:S(2)}, u32[]{:S(2)}) async-start(bf16[8,96,512]{2,1,0:T(8,128)(2,1)} %get-tuple-element.9), calls=%async_computation | async-start | bytes 1572864 | tf_op jit(solution)/shard_map/all_to_all | solution.py:233
  50.6 35.3 %copy-start = (bf16[512,4096]{1,0:T(8,128)(2,1)S(1)}, bf16[512,4096]{1,0:T(8,128)(2,1)}, u32[]{:S(2)}) copy-start(bf16[512,4096]{1,0:T(8,128)(2,1)} %weight.3) | copy-start | bytes 12582916
  86.5 12.4 %collective-permute-start = (bf16[4,96,512]{2,1,0:T(8,128)(2,1)S(1)}, bf16[4,96,512]{2,1,0:T(8,128)(2,1)S(1)}, u32[]{:S(2)}, u32[]{:S(2)}) collective-permute-start(bf16[4,96,512]{2,1,0:T(8,128)(2,1)S(1)} %get-tuple-element.12), channel_id=1, source_target_pairs={{0,1},{1,0},{2,3},{3,2},{4,5},{5,4},{6,7},{7,6},{8,9},{9,8},{10,11... | collective-permute-start | bytes 1179656 | tf_op jit(solution)/shard_map/ppermute | solution.py:273

commit v3 on v2

--- a/solution.py
+++ b/solution.py
@@ -16,8 +16,9 @@
 BIG = 2.0**100
 FLOOR = -1e29
 FAR = 1 << 30
-STAT = 16
-CHUNK = 512
+STAT = 8
+CHUNK = 256
+PEERS = 2
 SCALE = math.log2(math.e) / math.sqrt(HD)
 BF16 = jnp.bfloat16
 F32 = jnp.float32
@@ -63,7 +64,7 @@
         kv_out[rows, pl.ds(HD, HD)] = v[rows, :]
 
 
-def attend_kernel(place_in, docs_in, q, kv, out, place, docs, scores, values_t, keys, queries, sems):
+def attend_kernel(place_in, docs_in, q, kv, out, place, docs, scores, weights, values_t, keys, queries, sems):
     copies = [
         pltpu.make_async_copy(place_in, place, sems.at[0]),
         pltpu.make_async_copy(docs_in, docs, sems.at[1]),
@@ -119,36 +120,43 @@
 
     lax.fori_loop(0, n_blocks, key_columns, 0, unroll=4)
 
-    def one_peer(p, _):
-        for b in range(2):
-            q_pos = row + place[(p * z_size + my_z) * 2 + b] * BLOCK
-            doc = jnp.where((q_pos < begin) | (q_pos >= end), 1.0, 0.0)
-            block = jnp.where((q_pos >= begin - BLOCK) & (q_pos < begin), 1.0, 0.0)
-            later = jnp.where(q_pos < begin, 1.0, 0.0)
-            columns = jnp.where(wide < causal_at, doc, jnp.where(wide < own_at, block, later)).astype(BF16)
-            for h in range(heads):
-                rows = pl.ds((b * heads + h) * BLOCK, BLOCK)
-                queries[rows, pl.ds(0, HD)] = q[p, pl.ds(b * BLOCK, BLOCK), pl.ds(h * HD, HD)]
-                queries[rows, pl.ds(HD, HD)] = columns
-        top = jnp.full((8, lanes), -4.0 * BIG, F32)
-        for at in range(0, n_keys, CHUNK):
-            size = min(CHUNK, n_keys - at)
-            s = lax.dot_general(
-                keys[pl.ds(at, size), :],
-                queries[...],
-                (((1,), (1,)), ((), ())),
-                preferred_element_type=F32,
-            )
-            scores[pl.ds(at, size), :] = s
-            top = jnp.maximum(top, jnp.max(s.reshape(size // 8, 8, lanes), axis=0))
-        top = jnp.max(top, axis=0, keepdims=True)
-        safe = jnp.maximum(top, FLOOR)
-        sums = jnp.zeros((HD + STAT, lanes), F32)
-        for at in range(0, n_keys, CHUNK):
-            size = min(CHUNK, n_keys - at)
-            weights = jnp.exp2((scores[pl.ds(at, size), :] - safe) * SCALE).astype(BF16)
-            sums = sums + jnp.dot(values_t[:, pl.ds(at, size)], weights, preferred_element_type=F32)
-        out[p, pl.ds(0, HD), :] = sums[:HD].astype(BF16)
+    groups = peers // PEERS
+    wide_lanes = PEERS * lanes
+    starts = list(range(0, n_keys, CHUNK))
+
+    def set_queries(g):
+        for i in range(PEERS):
+            p = g * PEERS + i
+            for b in range(2):
+                q_pos = row + place[(p * z_size + my_z) * 2 + b] * BLOCK
+                doc = jnp.where((q_pos < begin) | (q_pos >= end), 1.0, 0.0)
+                block = jnp.where((q_pos >= begin - BLOCK) & (q_pos < begin), 1.0, 0.0)
+                later = jnp.where(q_pos < begin, 1.0, 0.0)
+                columns = jnp.where(wide < causal_at, doc, jnp.where(wide < own_at, block, later)).astype(BF16)
+                for h in range(heads):
+                    rows = pl.ds(((i * 2 + b) * heads + h) * BLOCK, BLOCK)
+                    queries[g % 2, rows, pl.ds(0, HD)] = q[p, pl.ds(b * BLOCK, BLOCK), pl.ds(h * HD, HD)]
+                    queries[g % 2, rows, pl.ds(HD, HD)] = columns
+
+    def score(g, at, top):
+        size = min(CHUNK, n_keys - at)
+        s = lax.dot_general(
+            keys[pl.ds(at, size), :],
+            queries[g % 2],
+            (((1,), (1,)), ((), ())),
+            preferred_element_type=F32,
+        )
+        scores[g % 2, pl.ds(at, size), :] = s
+        return jnp.maximum(top, jnp.max(s.reshape(size // 8, 8, wide_lanes), axis=0))
+
+    def weigh(g, at, safe):
+        size = min(CHUNK, n_keys - at)
+        w = jnp.exp2((scores[g % 2, pl.ds(at, size), :] - safe) * SCALE)
+        weights[g % 2, pl.ds(at, size), :] = w.astype(BF16)
+
+    def finish(g, top):
+        sums = jnp.dot(values_t[...], weights[g % 2], preferred_element_type=F32)
+        mixed = sums[:HD].astype(BF16)
         total = sums[HD : HD + 1]
         t0 = total.astype(BF16)
         t1 = (total - t0.astype(F32)).astype(BF16)
@@ -156,11 +164,29 @@
         rest = top - m0.astype(F32)
         m1 = rest.astype(BF16)
         m2 = (rest - m1.astype(F32)).astype(BF16)
-        zero = jnp.zeros((STAT - 5, lanes), BF16)
-        out[p, pl.ds(HD, STAT), :] = jnp.concatenate([m0, m1, m2, t0, t1, zero], axis=0)
-        return 0
-
-    lax.fori_loop(0, peers, one_peer, 0)
+        zero = jnp.zeros((STAT - 5, wide_lanes), BF16)
+        stat = jnp.concatenate([m0, m1, m2, t0, t1, zero], axis=0)
+        for i in range(PEERS):
+            out[g * PEERS + i, pl.ds(0, HD), :] = mixed[:, i * lanes : (i + 1) * lanes]
+            out[g * PEERS + i, pl.ds(HD, STAT), :] = stat[:, i * lanes : (i + 1) * lanes]
+
+    tops = {}
+    for step in range(groups + 2):
+        now, last, done = step, step - 1, step - 2
+        if now < groups:
+            set_queries(now)
+            top = jnp.full((8, wide_lanes), -4.0 * BIG, F32)
+        if 0 <= last < groups:
+            safe = jnp.maximum(tops[last], FLOOR)
+        for at in starts:
+            if now < groups:
+                top = score(now, at, top)
+            if 0 <= last < groups:
+                weigh(last, at, safe)
+        if 0 <= done:
+            finish(done, tops[done])
+        if now < groups:
+            tops[now] = jnp.max(top, axis=0, keepdims=True)
 
 
 def combine_kernel(parts, weight, rows, given):
@@ -242,13 +268,14 @@
         scratch_shapes=[
             pltpu.SMEM((n_place,), jnp.int32),
             pltpu.SMEM((n_docs,), jnp.int32),
-            pltpu.VMEM((n_keys, lanes), F32),
+            pltpu.VMEM((2, n_keys, PEERS * lanes), F32),
+            pltpu.VMEM((2, n_keys, PEERS * lanes), BF16),
             pltpu.VMEM((HD + STAT, n_keys), BF16),
             pltpu.VMEM((n_keys, 2 * HD), BF16),
-            pltpu.VMEM((lanes, 2 * HD), BF16),
+            pltpu.VMEM((2, PEERS * lanes, 2 * HD), BF16),
             pltpu.SemaphoreType.DMA((2,)),
         ],
-        compiler_params=pltpu.CompilerParams(vmem_limit_bytes=16 << 20),
+        compiler_params=pltpu.CompilerParams(vmem_limit_bytes=28 << 20),
         cost_estimate=pl.CostEstimate(flops=4 * pairs * HD, bytes_accessed=4 << 20, transcendentals=pairs),
         name="attend",
     )(

time: 111 us -> 105 us (0.946)
  Pallas kernels: 15.1 us -> 10.3 us
    pallas_call x1, Pallas kernels: 11.8 us -> 7.05 us  [body(): pl.pallas_call(attend_kernel, out_shape=jax.ShapeDtypeStruct((ny, HD + ST...]
where the time goes in v3:
time: 105 us
  blocking collectives  74.5 us (71%)
  starting transfers between devices  18.5 us (18%)
  Pallas kernels  10.3 us (10%)
    all_gather x1, blocking collectives, body(): kv_all = lax.all_gather(kv, 'z', axis=0, tiled=True)  40.8 us
    all_to_all x1, blocking collectives, body(): parts = lax.all_to_all(parts, 'y', split_axis=0, concat_axis=0, tiled=True)  22.6 us
    all_to_all x1, blocking collectives, body(): arrived = lax.all_to_all(both, 'x', split_axis=0, concat_axis=0, tiled=True)  11 us
    ppermute x1, starting transfers between devices, body(): got = lax.ppermute(given, 'c', [(0, 1), (1, 0)])  10.8 us
    all_to_all x1, starting transfers between devices, body(): q_all = lax.all_to_all(q_rot, 'y', split_axis=0, concat_axis=0, tiled=True)  7.65 us
    pallas_call x1, Pallas kernels, body(): pl.pallas_call(attend_kernel, out_shape=jax.ShapeDtypeStruct((ny, HD + ST...  7.05 us
    pallas_call x1, Pallas kernels, body(): pl.pallas_call(rotate_kernel, out_shape=(jax.ShapeDtypeStruct((ny, tok, q...  2.1 us
  transfers between devices with their start and end apart: 2, of which 1 were waited for; matrix products, arithmetic and copies ran while one was open for 0% of the time, Pallas kernels for 0%

profile of v3, /device:TPU:1, one launch (start us, length us, event | category | flops | bytes accessed | tf_op | source)
XLA Modules:
  0.0 105.0 jit_solution(4615804388804253600)
XLA Ops:
  0.0 2.1 %rotate.1 = (bf16[8,96,512]{2,1,0:T(8,128)(2,1)}, bf16[96,256]{1,0:T(8,128)(2,1)S(1)}) custom-call(s32[256]{0:T(256)} %place_in.3, bf16[96,512]{1,0:T(8,128)(2,1)} %q_in.1, bf16[96,128]{1,0:T(8,128)(2,1)} %k_in.1, bf16[96,128]{1,0:T(8,128)(2,1)} %v_in.1, f32[608,128]{1,0:T(8,128)} %constant.5.clone.table_in), custom_call_target="tpu_custom_call" | custom-call | tf_op jit(solution)/shard_map/rotate/pallas_call | solution.py:243
  2.1 7.7 %all-to-all-start = ((bf16[8,96,512]{2,1,0:T(8,128)(2,1)}), bf16[8,96,512]{2,1,0:T(8,128)(2,1)S(1)}, u32[]{:S(2)}, u32[]{:S(2)}) async-start(bf16[8,96,512]{2,1,0:T(8,128)(2,1)} %get-tuple-element.9), calls=%async_computation | async-start | bytes 1572864 | tf_op jit(solution)/shard_map/all_to_all | solution.py:259
  9.8 40.8 %all_gather.3.kv = bf16[1536,256]{1,0:T(8,128)(2,1)S(1)} all-gather(bf16[96,256]{1,0:T(8,128)(2,1)S(1)} %get-tuple-element.10), channel_id=1, replica_groups=mesh['y'=8,'z'=16,'x'=4,'c'=2] {'z'}, dimensions={0}, use_global_device_ids=true | all-gather | bytes 835584 | tf_op jit(solution)/shard_map/all_gather | solution.py:260
  50.6 0.0 all-to-all-done.q
  50.6 0.0 copy-start
  50.6 7.0 %attend.1 = bf16[8,136,384]{2,1,0:T(8,128)(2,1)S(1)} custom-call(s32[256]{0:T(256)} %place_in.3, s32[16]{0:T(128)} %docs_in.1, bf16[8,96,512]{2,1,0:T(8,128)(2,1)S(1)} %all-to-all-done.q, bf16[1536,256]{1,0:T(8,128)(2,1)S(1)} %all_gather.3.kv), custom_call_target="tpu_custom_call" | custom-call | flops 2415919104 | bytes 4194304 | tf_op jit(solution)/shard_map/attend/pallas_call | solution.py:263
  57.7 22.6 %all_to_all.15.parts = bf16[8,136,384]{2,1,0:T(8,128)(2,1)S(1)} all-to-all(bf16[8,136,384]{2,1,0:T(8,128)(2,1)S(1)} %attend.1), channel_id=1, replica_groups=mesh['y'=8,'z'=16,'x'=4,'c'=2] {'y'}, dimensions={0} | all-to-all | bytes 1671168 | tf_op jit(solution)/shard_map/all_to_all | solution.py:287
  80.3 0.0 copy-done
  80.3 0.7 combine.1
  81.0 10.8 %collective-permute-start = (bf16[4,96,512]{2,1,0:T(8,128)(2,1)S(1)}, bf16[4,96,512]{2,1,0:T(8,128)(2,1)S(1)}, u32[]{:S(2)}, u32[]{:S(2)}) collective-permute-start(bf16[4,96,512]{2,1,0:T(8,128)(2,1)S(1)} %get-tuple-element.12), channel_id=1, source_target_pairs={{0,1},{1,0},{2,3},{3,2},{4,5},{5,4},{6,7},{7,6},{8,9},{9,8},{10,11... | collective-permute-start | bytes 1179656 | tf_op jit(solution)/shard_map/ppermute | solution.py:300
  91.8 0.5 keep.1
  92.3 0.9 collective-permute-done
  93.2 0.1 add_convert_fusion
  93.3 11.0 %all_to_all.16 = bf16[4,96,512]{2,1,0:T(8,128)(2,1)S(1)} all-to-all(bf16[4,96,512]{2,1,0:T(8,128)(2,1)S(1)} %add_convert_fusion), channel_id=1, replica_groups=mesh['y'=8,'z'=16,'x'=4,'c'=2] {'x'}, dimensions={0} | all-to-all | bytes 786432 | tf_op jit(solution)/shard_map/all_to_all | solution.py:311
  104.3 0.7 reduce_sum.12
Async XLA Ops:
  2.1 48.5 %all-to-all-start = ((bf16[8,96,512]{2,1,0:T(8,128)(2,1)}), bf16[8,96,512]{2,1,0:T(8,128)(2,1)S(1)}, u32[]{:S(2)}, u32[]{:S(2)}) async-start(bf16[8,96,512]{2,1,0:T(8,128)(2,1)} %get-tuple-element.9), calls=%async_computation | async-start | bytes 1572864 | tf_op jit(solution)/shard_map/all_to_all | solution.py:259
  50.6 29.7 %copy-start = (bf16[512,4096]{1,0:T(8,128)(2,1)S(1)}, bf16[512,4096]{1,0:T(8,128)(2,1)}, u32[]{:S(2)}) copy-start(bf16[512,4096]{1,0:T(8,128)(2,1)} %weight.3) | copy-start | bytes 12582916
  81.0 12.2 %collective-permute-start = (bf16[4,96,512]{2,1,0:T(8,128)(2,1)S(1)}, bf16[4,96,512]{2,1,0:T(8,128)(2,1)S(1)}, u32[]{:S(2)}, u32[]{:S(2)}) collective-permute-start(bf16[4,96,512]{2,1,0:T(8,128)(2,1)S(1)} %get-tuple-element.12), channel_id=1, source_target_pairs={{0,1},{1,0},{2,3},{3,2},{4,5},{5,4},{6,7},{7,6},{8,9},{9,8},{10,11... | collective-permute-start | bytes 1179656 | tf_op jit(solution)/shard_map/ppermute | solution.py:300

commit v4 on v3

--- a/solution.py
+++ b/solution.py
@@ -17,7 +17,7 @@
 FLOOR = -1e29
 FAR = 1 << 30
 STAT = 8
-CHUNK = 256
+CHUNK = 384
 PEERS = 2
 SCALE = math.log2(math.e) / math.sqrt(HD)
 BF16 = jnp.bfloat16
@@ -32,12 +32,17 @@
     return np.concatenate([np.cos(row), np.sin(row), np.cos(start), np.sin(start)]).astype(np.float32)
 
 
-def rotate_kernel(place_in, q_in, k_in, v_in, table_in, q_out, kv_out, place, q, k, v, table, sems):
-    sources = (place_in, table_in, q_in, k_in, v_in)
-    copies = [pltpu.make_async_copy(s, d, sems.at[i]) for i, (s, d) in enumerate(zip(sources, (place, table, q, k, v)))]
+def rotate_kernel(
+    place_in, docs_in, q_in, k_in, v_in, table_in,
+    q_out, kv_out, place_out, docs_out,
+    place, q, k, v, table, turned, sems, out_sems,
+):
+    sources = (place_in, table_in, q_in, k_in, v_in, place_in, docs_in)
+    targets = (place, table, q, k, v, place_out, docs_out)
+    copies = [pltpu.make_async_copy(s, d, sems.at[i]) for i, (s, d) in enumerate(zip(sources, targets))]
     for copy in copies:
         copy.start()
-    for copy in copies:
+    for copy in copies[:3]:
         copy.wait()
     heads = q.shape[1] // HD
     blocks = place.shape[0]
@@ -45,23 +50,33 @@
     lane = lax.broadcasted_iota(jnp.int32, (BLOCK, HD), 1)
     cos_row = table[pl.ds(0, BLOCK), :]
     sin_row = table[pl.ds(BLOCK, BLOCK), :]
+    factors = []
     for b in range(2):
         at = place[first * 2 + b]
         c0 = table[pl.ds(2 * BLOCK + at, 1), :]
         s0 = table[pl.ds(2 * BLOCK + blocks + at, 1), :]
         cosine = c0 * cos_row - s0 * sin_row
         sine = s0 * cos_row + c0 * sin_row
-        sine = jnp.where(lane < HALF, -sine, sine)
+        factors.append((cosine, jnp.where(lane < HALF, -sine, sine)))
+    for b in range(2):
+        cosine, sine = factors[b]
         rows = pl.ds(b * BLOCK, BLOCK)
         for h in range(heads):
             x = q[rows, pl.ds(h * HD, HD)].astype(F32)
-            y = (x * cosine + pltpu.roll(x, HALF, 1) * sine).astype(BF16)
-            for p in range(q_out.shape[0]):
-                q_out[p, rows, pl.ds(h * HD, HD)] = y
+            turned[rows, pl.ds(h * HD, HD)] = (x * cosine + pltpu.roll(x, HALF, 1) * sine).astype(BF16)
+    sends = [pltpu.make_async_copy(turned, q_out.at[p], out_sems.at[p]) for p in range(q_out.shape[0])]
+    for send in sends:
+        send.start()
+    for copy in copies[3:]:
+        copy.wait()
+    for b in range(2):
+        cosine, sine = factors[b]
+        rows = pl.ds(b * BLOCK, BLOCK)
         x = k[rows, :].astype(F32)
-        y = x * cosine + pltpu.roll(x, HALF, 1) * sine
-        kv_out[rows, pl.ds(0, HD)] = y.astype(BF16)
+        kv_out[rows, pl.ds(0, HD)] = (x * cosine + pltpu.roll(x, HALF, 1) * sine).astype(BF16)
         kv_out[rows, pl.ds(HD, HD)] = v[rows, :]
+    for send in sends:
+        send.wait()
 
 
 def attend_kernel(place_in, docs_in, q, kv, out, place, docs, scores, weights, values_t, keys, queries, sems):
@@ -80,8 +95,6 @@
     z_size = lax.axis_size("z")
     my_y = lax.axis_index("y")
     my_z = lax.axis_index("z")
-    values_t[pl.ds(0, HD), :] = kv[:, pl.ds(HD, HD)].T
-    values_t[pl.ds(HD, STAT), :] = jnp.ones((STAT, n_keys), BF16)
     keys[:, pl.ds(0, HD)] = kv[:, pl.ds(0, HD)]
     for copy in copies:
         copy.wait()
@@ -111,14 +124,11 @@
     row = lax.broadcasted_iota(jnp.int32, (BLOCK, HD), 0)
     wide = lax.broadcasted_iota(jnp.int32, (BLOCK, HD), 1)
 
-    def key_columns(j, _):
-        k_pos = row + place[my_y * n_blocks + j] * BLOCK
-        inside = (k_pos >= begin) & (k_pos < end)
-        at = pl.multiple_of(j * BLOCK, BLOCK)
-        keys[pl.ds(at, BLOCK), pl.ds(HD, HD)] = jnp.where(inside, -BIG, 0.0).astype(BF16)
-        return 0
-
-    lax.fori_loop(0, n_blocks, key_columns, 0, unroll=4)
+    def key_columns(first, last):
+        for j in range(first, last):
+            k_pos = row + place[my_y * n_blocks + j] * BLOCK
+            inside = (k_pos >= begin) & (k_pos < end)
+            keys[pl.ds(j * BLOCK, BLOCK), pl.ds(HD, HD)] = jnp.where(inside, -BIG, 0.0).astype(BF16)
 
     groups = peers // PEERS
     wide_lanes = PEERS * lanes
@@ -179,10 +189,15 @@
         if 0 <= last < groups:
             safe = jnp.maximum(tops[last], FLOOR)
         for at in starts:
+            if now == 0:
+                key_columns(at // BLOCK, min(at + CHUNK, n_keys) // BLOCK)
             if now < groups:
                 top = score(now, at, top)
             if 0 <= last < groups:
                 weigh(last, at, safe)
+        if now == 0:
+            values_t[pl.ds(0, HD), :] = kv[:, pl.ds(HD, HD)].T
+            values_t[pl.ds(HD, STAT), :] = jnp.ones((STAT, n_keys), BF16)
         if 0 <= done:
             finish(done, tops[done])
         if now < groups:
@@ -240,22 +255,31 @@
     hbm = pl.BlockSpec(memory_space=pltpu.HBM)
     n_place = stretch_place.shape[0]
     n_docs = doc_lengths.shape[0]
-    q_rot, kv = pl.pallas_call(
+    n_inputs = 6
+    args = (stretch_place, doc_lengths, queries, keys, values, jnp.asarray(table))
+    q_rot, kv, place, docs = pl.pallas_call(
         rotate_kernel,
-        out_shape=(jax.ShapeDtypeStruct((ny, tok, q_width), BF16), jax.ShapeDtypeStruct((tok, 2 * HD), BF16)),
-        in_specs=[hbm] * 5,
-        out_specs=(vmem, vmem),
+        out_shape=(
+            jax.ShapeDtypeStruct((ny, tok, q_width), BF16),
+            jax.ShapeDtypeStruct((tok, 2 * HD), BF16),
+            jax.ShapeDtypeStruct((n_place,), jnp.int32),
+            jax.ShapeDtypeStruct((n_docs,), jnp.int32),
+        ),
+        in_specs=[hbm] * n_inputs,
+        out_specs=(hbm, vmem, vmem, vmem),
         scratch_shapes=[
             pltpu.SMEM((n_place,), jnp.int32),
             pltpu.VMEM((tok, q_width), BF16),
             pltpu.VMEM((tok, HD), BF16),
             pltpu.VMEM((tok, HD), BF16),
             pltpu.VMEM(table.shape, F32),
-            pltpu.SemaphoreType.DMA((5,)),
+            pltpu.VMEM((tok, q_width), BF16),
+            pltpu.SemaphoreType.DMA((n_inputs + 1,)),
+            pltpu.SemaphoreType.DMA((ny,)),
         ],
         compiler_params=pltpu.CompilerParams(vmem_limit_bytes=4 << 20),
         name="rotate",
-    )(*[pltpu.with_memory_space_constraint(a, pltpu.HBM) for a in (stretch_place, queries, keys, values, jnp.asarray(table))])
+    )(*[pltpu.with_memory_space_constraint(a, pltpu.HBM) for a in args])
     q_all = lax.all_to_all(q_rot, "y", split_axis=0, concat_axis=0, tiled=True)
     kv_all = lax.all_gather(kv, "z", axis=0, tiled=True)
     n_keys = nz * tok
@@ -263,7 +287,7 @@
     parts = pl.pallas_call(
         attend_kernel,
         out_shape=jax.ShapeDtypeStruct((ny, HD + STAT, lanes), BF16),
-        in_specs=[hbm, hbm, vmem, vmem],
+        in_specs=[vmem, vmem, vmem, vmem],
         out_specs=vmem,
         scratch_shapes=[
             pltpu.SMEM((n_place,), jnp.int32),
@@ -279,8 +303,8 @@
         cost_estimate=pl.CostEstimate(flops=4 * pairs * HD, bytes_accessed=4 << 20, transcendentals=pairs),
         name="attend",
     )(
-        pltpu.with_memory_space_constraint(stretch_place, pltpu.HBM),
-        pltpu.with_memory_space_constraint(doc_lengths, pltpu.HBM),
+        place,
+        docs,
         q_all,
         kv_all,
     )

time: 105 us -> 105 us (level)
  no operation moved by 1% of the time
where the time goes in v4:
time: 105 us
  blocking collectives  74.5 us (71%)
  starting transfers between devices  18.4 us (18%)
  Pallas kernels  9.86 us (9%)
    all_gather x1, blocking collectives, body(): kv_all = lax.all_gather(kv, 'z', axis=0, tiled=True)  40.8 us
    all_to_all x1, blocking collectives, body(): parts = lax.all_to_all(parts, 'y', split_axis=0, concat_axis=0, tiled=True)  22.7 us
    all_to_all x1, blocking collectives, body(): arrived = lax.all_to_all(both, 'x', split_axis=0, concat_axis=0, tiled=True)  11 us
    ppermute x1, starting transfers between devices, body(): got = lax.ppermute(given, 'c', [(0, 1), (1, 0)])  10.8 us
    all_to_all x1, starting transfers between devices, body(): q_all = lax.all_to_all(q_rot, 'y', split_axis=0, concat_axis=0, tiled=True)  7.65 us
    pallas_call x1, Pallas kernels, body(): pl.pallas_call(attend_kernel, out_shape=jax.ShapeDtypeStruct((ny, HD + ST...  6.58 us
    pallas_call x1, Pallas kernels, body(): pl.pallas_call(rotate_kernel, out_shape=(jax.ShapeDtypeStruct((ny, tok, q...  2.1 us
  transfers between devices with their start and end apart: 2, of which 1 were waited for; matrix products, arithmetic and copies ran while one was open for 0% of the time, Pallas kernels for 0%

profile of v4, /device:TPU:1, one launch (start us, length us, event | category | flops | bytes accessed | tf_op | source)
XLA Modules:
  0.0 104.6 jit_solution(15448629920341935272)
XLA Ops:
  0.0 2.1 %rotate.1 = (bf16[8,96,512]{2,1,0:T(8,128)(2,1)}, bf16[96,256]{1,0:T(8,128)(2,1)S(1)}, s32[256]{0:T(256)S(1)}, s32[16]{0:T(128)S(1)}) custom-call(s32[256]{0:T(256)} %place_in.1, s32[16]{0:T(128)} %docs_in.1, bf16[96,512]{1,0:T(8,128)(2,1)} %q_in.1, bf16[96,128]{1,0:T(8,128)(2,1)} %k_in.1, bf16[96,128]{1,0:T(8,128)(2,1)} %v_in.1, ...), custom_call_target="tpu_custom_call" | custom-call | tf_op jit(solution)/shard_map/rotate/pallas_call | solution.py:260
  2.1 7.7 %all-to-all-start = ((bf16[8,96,512]{2,1,0:T(8,128)(2,1)}), bf16[8,96,512]{2,1,0:T(8,128)(2,1)S(1)}, u32[]{:S(2)}, u32[]{:S(2)}) async-start(bf16[8,96,512]{2,1,0:T(8,128)(2,1)} %get-tuple-element.13), calls=%async_computation | async-start | bytes 1572864 | tf_op jit(solution)/shard_map/all_to_all | solution.py:283
  9.8 40.8 %all_gather.3.kv = bf16[1536,256]{1,0:T(8,128)(2,1)S(1)} all-gather(bf16[96,256]{1,0:T(8,128)(2,1)S(1)} %get-tuple-element.14), channel_id=1, replica_groups=mesh['y'=8,'z'=16,'x'=4,'c'=2] {'z'}, dimensions={0}, use_global_device_ids=true | all-gather | bytes 835584 | tf_op jit(solution)/shard_map/all_gather | solution.py:284
  50.6 0.0 all-to-all-done.q
  50.6 0.0 copy-start
  50.6 6.6 %attend.1 = bf16[8,136,384]{2,1,0:T(8,128)(2,1)S(1)} custom-call(s32[256]{0:T(256)S(1)} %get-tuple-element.11.place_in, s32[16]{0:T(128)S(1)} %get-tuple-element.12.docs_in, bf16[8,96,512]{2,1,0:T(8,128)(2,1)S(1)} %all-to-all-done.q, bf16[1536,256]{1,0:T(8,128)(2,1)S(1)} %all_gather.3.kv), custom_call_target="tpu_custom_call" | custom-call | flops 2415919104 | bytes 4194304 | tf_op jit(solution)/shard_map/attend/pallas_call | solution.py:287
  57.2 22.7 %all_to_all.15.parts = bf16[8,136,384]{2,1,0:T(8,128)(2,1)S(1)} all-to-all(bf16[8,136,384]{2,1,0:T(8,128)(2,1)S(1)} %attend.1), channel_id=1, replica_groups=mesh['y'=8,'z'=16,'x'=4,'c'=2] {'y'}, dimensions={0} | all-to-all | bytes 1671168 | tf_op jit(solution)/shard_map/all_to_all | solution.py:311
  79.9 0.0 copy-done
  79.9 0.7 combine.1
  80.6 10.8 %collective-permute-start = (bf16[4,96,512]{2,1,0:T(8,128)(2,1)S(1)}, bf16[4,96,512]{2,1,0:T(8,128)(2,1)S(1)}, u32[]{:S(2)}, u32[]{:S(2)}) collective-permute-start(bf16[4,96,512]{2,1,0:T(8,128)(2,1)S(1)} %get-tuple-element.16), channel_id=1, source_target_pairs={{0,1},{1,0},{2,3},{3,2},{4,5},{5,4},{6,7},{7,6},{8,9},{9,8},{10,11... | collective-permute-start | bytes 1179656 | tf_op jit(solution)/shard_map/ppermute | solution.py:324
  91.4 0.5 keep.1
  91.9 0.8 collective-permute-done
  92.7 0.1 add_convert_fusion
  92.8 11.0 %all_to_all.16 = bf16[4,96,512]{2,1,0:T(8,128)(2,1)S(1)} all-to-all(bf16[4,96,512]{2,1,0:T(8,128)(2,1)S(1)} %add_convert_fusion), channel_id=1, replica_groups=mesh['y'=8,'z'=16,'x'=4,'c'=2] {'x'}, dimensions={0} | all-to-all | bytes 786432 | tf_op jit(solution)/shard_map/all_to_all | solution.py:335
  103.9 0.7 reduce_sum.12
Async XLA Ops:
  2.1 48.5 %all-to-all-start = ((bf16[8,96,512]{2,1,0:T(8,128)(2,1)}), bf16[8,96,512]{2,1,0:T(8,128)(2,1)S(1)}, u32[]{:S(2)}, u32[]{:S(2)}) async-start(bf16[8,96,512]{2,1,0:T(8,128)(2,1)} %get-tuple-element.13), calls=%async_computation | async-start | bytes 1572864 | tf_op jit(solution)/shard_map/all_to_all | solution.py:283
  50.6 29.3 %copy-start = (bf16[512,4096]{1,0:T(8,128)(2,1)S(1)}, bf16[512,4096]{1,0:T(8,128)(2,1)}, u32[]{:S(2)}) copy-start(bf16[512,4096]{1,0:T(8,128)(2,1)} %weight.3) | copy-start | bytes 12582916
  80.6 12.1 %collective-permute-start = (bf16[4,96,512]{2,1,0:T(8,128)(2,1)S(1)}, bf16[4,96,512]{2,1,0:T(8,128)(2,1)S(1)}, u32[]{:S(2)}, u32[]{:S(2)}) collective-permute-start(bf16[4,96,512]{2,1,0:T(8,128)(2,1)S(1)} %get-tuple-element.16), channel_id=1, source_target_pairs={{0,1},{1,0},{2,3},{3,2},{4,5},{5,4},{6,7},{7,6},{8,9},{9,8},{10,11... | collective-permute-start | bytes 1179656 | tf_op jit(solution)/shard_map/ppermute | solution.py:324
